TPU v7x, 32 devices: a whole 2x2x4 slice. The times are simulated.
32 devices in a mesh: lat: 4 (over y, core), lon: 8 (over z, x).
Axes of the slice: x: 2, y: 2, z: 4, core: 2. Of those that a mesh axis runs over, the one named last changes fastest.
Arguments:
- coarse: bfloat16 [30720, 1104], P(('lat', 'lon')), may hold values from -6 to 6
- w_mix: bfloat16 [69, 64], replicated, may hold values from -0.75 to 0.75
- interp: bfloat16 [16, 256], replicated, may hold values from -1.5 to 1.5
- kernel: bfloat16 [3, 3, 64, 64], replicated, may hold values from -0.25 to 0.25
- bias: float32 [64], replicated, may hold values from -3 to 3
- block_ids: int32 [32, 144], replicated, may hold values from 0 to 30719, as said below
- valid: int32 [32, 144], replicated, may hold values from 0 to 1, as said below
Outputs:
- fine_out: bfloat16 [64, 1152, 1024], P(None, 'lat', 'lon')
Inputs may be any that keep to these rules, and one draw needn't show every extreme that they name: `block_ids`: the coarse grid has 96 block rows and 320 block columns, held block-cyclically: block (r, c) is row ((r mod 4) * 8 + c mod 8) * 960 + (r div 4) * 40 + c div 8 of coarse. Slot p of tile t holds block (r0 + (t div 8) * 18 + p div 8, (c0 + (t mod 8) * 8 + p mod 8) mod (320)), with offsets r0 and c0 common to all tiles. Among the valid slots of one tile at most 5 name blocks of one device, and in every tile exactly 5 valid slots name blocks of some one device. Every tile has 5 or more valid slots.
All inputs are finite; a program needn't handle non-finite values.
Results may differ from a plain program's by a relative error of at most 0.0055.
Values may be sent and summed in bfloat16 or wider, within the bound.
A program may use at most 192 MiB of HBM per device.

v0:
```python
import functools

import jax
import jax.numpy as jnp
from jax import lax
from jax.experimental import pallas as pl
from jax.experimental.pallas import tpu as pltpu
from jax.sharding import PartitionSpec as P

PR = 18
PC = 8
SIDE = 16
STEPS = 3


def exchange(n_dev, n_lon, out_ref, in_ref, send_sem, recv_sem, own_sem):
    me = lax.axis_index("lat") * n_lon + lax.axis_index("lon")

    def copy(d):
        target = lax.rem(me + d, n_dev)
        return pltpu.make_async_remote_copy(
            src_ref=out_ref.at[target],
            dst_ref=in_ref.at[me],
            send_sem=send_sem.at[d],
            recv_sem=recv_sem.at[d],
            device_id={"lat": target // n_lon, "lon": lax.rem(target, n_lon)},
            device_id_type=pl.DeviceIdType.MESH,
        )

    own = pltpu.make_async_copy(out_ref.at[me], in_ref.at[me], own_sem)

    @pl.loop(1, n_dev)
    def _(d):
        copy(d).start()

    own.start()

    @pl.loop(1, n_dev)
    def _(d):
        copy(d).wait()

    own.wait()


def all_to_all(outgoing, n_lat, n_lon):
    n_dev = n_lat * n_lon
    return pl.pallas_call(
        functools.partial(exchange, n_dev, n_lon),
        out_shape=jax.ShapeDtypeStruct(outgoing.shape, outgoing.dtype),
        in_specs=[pl.BlockSpec(memory_space=pl.ANY)],
        out_specs=pl.BlockSpec(memory_space=pl.ANY),
        scratch_shapes=[
            pltpu.SemaphoreType.DMA((n_dev,)),
            pltpu.SemaphoreType.DMA((n_dev,)),
            pltpu.SemaphoreType.DMA,
        ],
        compiler_params=pltpu.CompilerParams(has_side_effects=True),
        name="exchange",
    )(outgoing)


NT = (((1,), (1,)), ((), ()))


def build_maps(interp, rhs, up, down):
    f32, bf16 = jnp.float32, jnp.bfloat16
    rows = SIDE * PC
    breadth = SIDE * PC
    row = lax.broadcasted_iota(jnp.int32, (rows, breadth), 0)
    lane = lax.broadcasted_iota(jnp.int32, (rows, breadth), 1)
    pick_k = lax.broadcasted_iota(jnp.int32, (rows, SIDE), 0) // PC
    pick_k = (pick_k == lax.broadcasted_iota(jnp.int32, (rows, SIDE), 1)).astype(bf16)
    repeated = jnp.dot(pick_k, interp, preferred_element_type=f32).astype(bf16)
    lane_from = lax.broadcasted_iota(jnp.int32, (SIDE, breadth), 0)
    lane_to = lax.broadcasted_iota(jnp.int32, (SIDE, breadth), 1)
    spread = (lane_from == lane_to % SIDE).astype(bf16)
    pc = row % PC
    own = [
        (lane > 0) & (pc == (lane - 1) // SIDE),
        pc == lane // SIDE,
        pc == (lane + 1) // SIDE,
    ]
    side, dy_of = pc // 4, pc % 4
    rhs[...] = jnp.zeros_like(rhs)
    up[...] = jnp.zeros_like(up)
    down[...] = jnp.zeros_like(down)

    def place(fy):
        if fy == 0:
            return SIDE // 2 - 1, breadth
        return (fy - 1) // 2, ((fy - 1) % 2) * breadth

    halo = [[None] * SIDE for _ in range(3)]
    for r in range(SIDE):
        flat = jnp.dot(repeated[:, r * SIDE:(r + 1) * SIDE], spread, preferred_element_type=f32)
        after = pltpu.roll(flat, 1, 1)
        before = pltpu.roll(flat, breadth - 1, 1)
        taps = [
            jnp.where(own[d], v, 0.0).astype(bf16) for d, v in enumerate((after, flat, before))
        ]
        edge = jnp.where((lane == 0) & (side == 0), after, 0.0)
        edge = edge + jnp.where((lane == breadth - 1) & (side == 1), before, 0.0)
        for dy in range(3):
            fy = r + 1 - dy
            part = jnp.where(dy_of == dy, edge, 0.0)
            if 0 <= fy < SIDE:
                pair, at = place(fy)
                for dx in range(3):
                    tap = (dy * 3 + dx) * rows
                    rhs[pair, tap:tap + rows, at:at + breadth] = taps[dx]
                halo[dy][fy] = part
            elif fy == SIDE:
                for dx in range(3):
                    up[dx * rows:(dx + 1) * rows, breadth:] = taps[dx]
                up[3 * rows:, breadth:] = part.astype(bf16)
            else:
                for dx in range(3):
                    down[dx * rows:(dx + 1) * rows, :breadth] = taps[dx]
                down[3 * rows:, :breadth] = part.astype(bf16)
    for fy in range(SIDE):
        pair, at = place(fy)
        total = sum(halo[dy][fy] for dy in range(3) if halo[dy][fy] is not None)
        rhs[pair, 9 * rows:, at:at + breadth] = total.astype(bf16)


def build_left(arrived, source, w_mix, kernel, grouped, left):
    f32, bf16 = jnp.float32, jnp.bfloat16
    rows = SIDE * PC
    high = PR + 2
    c_in = arrived.shape[1] // SIDE
    c_out = kernel.shape[0] // 9
    slots = lax.broadcasted_iota(jnp.int32, (source.shape[0], arrived.shape[0]), 1)
    pick = (slots == source[...]).astype(f32).astype(bf16)
    window = jnp.dot(pick, arrived[...], preferred_element_type=f32)
    grouped[...] = jnp.zeros_like(grouped)
    for k in range(SIDE):
        cell = window[:, k * c_in:(k + 1) * c_in]
        grouped[:, 0, k, :, :c_in] = cell[:high * PC].reshape(high, PC, c_in)
        grouped[:, 1, k, :, :c_in] = cell[high * PC:].reshape(high, PC, c_in)
    both = lax.dot_general(kernel[...], w_mix[...], NT, preferred_element_type=f32).astype(bf16)
    lane = lax.broadcasted_iota(jnp.int32, (c_out, rows), 1) % PC

    @pl.loop(0, high)
    def _(wr):
        cells = grouped[wr].reshape(2 * rows, 128).astype(bf16)
        res = lax.dot_general(both, cells, NT, preferred_element_type=f32)
        at = pl.ds(pl.multiple_of(wr * c_out, c_out), c_out)
        edge = jnp.zeros((c_out, rows), f32)
        for tap in range(9):
            part = res[tap * c_out:(tap + 1) * c_out]
            left[at, tap * rows:(tap + 1) * rows] = part[:, :rows].astype(bf16)
            dy, dx = divmod(tap, 3)
            if dx != 1:
                edge = jnp.where(lane == (dx // 2) * 4 + dy, part[:, rows:], edge)
        left[at, 9 * rows:] = edge.astype(bf16)


def convolve(arrived, source, w_mix, interp, kernel, bias, land, out, grouped, left, rhs, up, down, fine):
    f32 = jnp.float32
    rows = SIDE * PC
    c_out = kernel.shape[0] // 9
    step = pl.program_id(0)
    count = PR // STEPS
    many = count * c_out

    @pl.when(step == 0)
    def _():
        build_maps(interp[...], rhs, up, down)
        build_left(arrived, source, w_mix, kernel, grouped, left)

    base = pl.multiple_of(step * many, c_out)
    above = pl.ds(base, many)
    here = pl.ds(pl.multiple_of(base + c_out, c_out), many)
    below = pl.ds(pl.multiple_of(base + 2 * c_out, c_out), many)
    mask = land[step]
    pairs = SIDE // 2

    def put(total, fys):
        for half, fy in enumerate(fys):
            part = total[:, half * rows:(half + 1) * rows].reshape(count, c_out, rows)
            part = (part + bias[...][None]) * mask[:, None, :]
            fine[pl.ds(fy, many, stride=SIDE), :] = part.reshape(many, rows)

    for pair in range(pairs):
        total = jnp.dot(left[here, :], rhs[pair], preferred_element_type=f32)
        if pair == pairs - 1:
            total += jnp.dot(left[above, :3 * rows], up[:3 * rows], preferred_element_type=f32)
            total += jnp.dot(left[above, 9 * rows:], up[3 * rows:], preferred_element_type=f32)
            total += jnp.dot(left[below, 6 * rows:9 * rows], down[:3 * rows], preferred_element_type=f32)
            total += jnp.dot(left[below, 9 * rows:], down[3 * rows:], preferred_element_type=f32)
            put(total, (SIDE - 1, 0))
        else:
            put(total, (2 * pair + 1, 2 * pair + 2))
    for pr in range(count):
        block = fine[pr * c_out * SIDE:(pr + 1) * c_out * SIDE, :]
        out[:, pr * SIDE:(pr + 1) * SIDE, :] = block.reshape(c_out, SIDE, rows).astype(out.dtype)


def per_device(coarse, w_mix, interp, kernel, bias, block_ids, valid):
    n_lat = lax.axis_size("lat")
    n_lon = lax.axis_size("lon")
    n_dev = n_lat * n_lon
    lat, lon = lax.axis_index("lat"), lax.axis_index("lon")
    held = coarse.shape[0]
    channels = w_mix.shape[1]
    high, wide = PR + 2, PC + 2
    per_col = -(-wide // n_lon)
    most = -(-(-(-high // n_lat) * per_col) // 16) * 16
    i32 = jnp.int32
    first = block_ids[0, 0]
    cols = block_ids[0, n_lat * PC] - first
    spot, holder = first % held, first // held
    r0 = (spot // cols) * n_lat + holder // n_lon
    c0 = (spot % cols) * n_lon + holder % n_lon

    tile = jnp.arange(n_dev, dtype=i32)[:, None]
    place = jnp.arange(most, dtype=i32)[None, :]
    row_from = r0 + (tile // n_lon) * PR - 1
    col_from = c0 + (tile % n_lon) * PC - 1
    row = row_from + jnp.mod(lat - row_from, n_lat) + (place // per_col) * n_lat
    col = col_from + jnp.mod(lon - col_from, n_lon) + (place % per_col) * n_lon
    table = jnp.floor_divide(row, n_lat) * cols + jnp.mod(col, cols * n_lon) // n_lon
    outgoing = coarse[jnp.clip(table, 0, held - 1).reshape(-1)]
    arrived = all_to_all(outgoing.reshape(n_dev, most, coarse.shape[1]), n_lat, n_lon)

    image = valid.reshape(n_lat, n_lon, PR, PC).transpose(0, 2, 1, 3)
    image = jnp.pad(image.reshape(n_lat * PR, n_lon * PC), 1)
    live = lax.dynamic_slice(image, (lat * PR, lon * PC), (high, wide))
    wr = jnp.arange(high, dtype=i32)[:, None]
    wc = jnp.arange(wide, dtype=i32)[None, :]
    owner = jnp.mod(r0 + lat * PR - 1 + wr, n_lat) * n_lon
    owner = owner + jnp.mod(c0 + lon * PC - 1 + wc, n_lon)
    rank = (wr // n_lat) * per_col + wc // n_lon
    source = jnp.where(live > 0, owner * most + rank, -1)
    edges = jnp.repeat(source[:, ::wide - 1], 4, axis=1)
    source = jnp.concatenate([source[:, 1:-1].reshape(-1), edges.reshape(-1)])[:, None]
    land = jnp.repeat(live[1:-1, 1:-1].astype(jnp.float32), SIDE, axis=1)

    rows = SIDE * PC
    full = lambda *shape: pl.BlockSpec(shape, lambda i: (0,) * len(shape))
    arrived = arrived.reshape(n_dev * most, coarse.shape[1])
    count = PR // STEPS
    taps = kernel.reshape(9 * channels, channels)
    mixer = jnp.pad(w_mix, ((0, 128 - w_mix.shape[0]), (0, 0)))
    return pl.pallas_call(
        convolve,
        grid=(STEPS,),
        out_shape=jax.ShapeDtypeStruct((channels, PR * SIDE, rows), jnp.bfloat16),
        in_specs=[
            full(*arrived.shape), full(*source.shape), full(*mixer.shape), full(*interp.shape),
            full(*taps.shape), full(channels, 1), full(STEPS, count, rows),
        ],
        out_specs=pl.BlockSpec((channels, count * SIDE, rows), lambda i: (0, i, 0)),
        scratch_shapes=[
            pltpu.VMEM((high, 2, SIDE, PC, 128), jnp.float32),
            pltpu.VMEM((high * channels, 10 * rows), jnp.bfloat16),
            pltpu.VMEM((SIDE // 2, 10 * rows, 2 * rows), jnp.bfloat16),
            pltpu.VMEM((4 * rows, 2 * rows), jnp.bfloat16),
            pltpu.VMEM((4 * rows, 2 * rows), jnp.bfloat16),
            pltpu.VMEM((count * channels * SIDE, rows), jnp.float32),
        ],
        compiler_params=pltpu.CompilerParams(vmem_limit_bytes=60 * 1024 * 1024),
        name="convolve",
    )(arrived, source, mixer, interp, taps, bias[:, None], land.reshape(STEPS, count, rows))


def solution(mesh):
    placed = (P(("lat", "lon"), None), P(), P(), P(), P(), P(), P())
    return jax.shard_map(
        per_device, mesh=mesh, in_specs=placed, out_specs=P(None, "lat", "lon"), check_vma=False
    )
```

profile of v0, /device:TPU:0, one launch (start us, length us, event | category | flops | bytes accessed | tf_op | source)
XLA Modules:
  0.0 71.7 jit_solution(2097974044852167255)
XLA Ops:
  0.0 0.0 copy-start
  0.0 1.4 %fusion.18 = (s32[1,1]{1,0:T(1,128)}, s32[1,1]{1,0:T(1,128)}) fusion(s32[32,144]{1,0:T(8,128)} %param.12), kind=kLoop, calls=%fused_computation.66 | loop fusion | bytes 16 | tf_op jit(solution)/shard_map/slice | solution.py:210
  4.9 0.3 add_remainder_fusion
  5.1 0.1 rem.247
  5.2 0.1 broadcast_add_fusion
  5.3 0.1 add.336
  5.4 0.8 %copy.14 = bf16[69,64]{1,0:T(8,128)(2,1)S(1)} copy(bf16[69,64]{0,1:T(8,128)(2,1)} %param.8) | data formatting | bytes 17664 | tf_op args[1]
  6.3 0.6 pad.9.w_mix
  6.9 1.3 %copy.17.bias = f32[64,1]{1,0:T(8,128)} copy(f32[64,1]{0,1:T(1,128)} %bitcast.19) | data formatting | bytes 512 | tf_op jit(solution)/shard_map/broadcast_in_dim | solution.py:264
  8.2 0.9 %copy.10 = s32[32,144]{0,1:T(8,128)S(1)} copy(s32[32,144]{1,0:T(8,128)} %param.13) | data formatting | bytes 36864 | tf_op args[6]
  9.1 0.2 reshape.484
  9.3 0.3 copy.11
  9.6 0.1 reshape.485
  9.7 0.1 fusion.1
  9.8 0.1 add_select_fusion
  9.9 0.1 copy.12
  10.0 0.1 reshape.486
  10.1 0.1 copy.15
  10.2 0.1 copy.13
  10.3 0.1 broadcast_in_dim.22
  10.3 0.1 reshape_reshape.6
  10.5 0.1 pad_add_fusion
  10.5 0.1 broadcast_in_dim.25
  10.6 0.7 reshape_reshape.7.land
  11.3 0.8 %broadcast_in_dim.26.source = s32[320,1]{1,0:T(8,128)} reshape(s32[320]{0:T(512)S(1)} %pad_add_fusion) | data formatting | bytes 2560 | tf_op jit(solution)/shard_map/broadcast_in_dim | solution.py:236
  12.1 0.0 copy-done
  12.1 2.8 %gather_fusion = bf16[512,1104]{1,0:T(8,128)(2,1)} fusion(bf16[960,1104]{1,0:T(8,128)(2,1)S(1)} %copy-done, s32[1024]{0:T(1024)S(1)} %pad_clamp_fusion), kind=kCustom, calls=%fused_computation | custom fusion | bytes 2263040 | tf_op jit(solution)/shard_map/gather | solution.py:223
  14.9 36.2 %exchange.1 = bf16[32,16,1104]{2,1,0:T(8,128)(2,1)} custom-call(bf16[32,16,1104]{2,1,0:T(8,128)(2,1)} %bitcast.15), custom_call_target="tpu_custom_call" | custom-call | tf_op jit(solution)/shard_map/exchange/pallas_call | solution.py:47
  51.1 20.6 %convolve.1 = bf16[64,288,128]{2,1,0:T(8,128)(2,1)} custom-call(bf16[512,1104]{1,0:T(8,128)(2,1)} %bitcast.14, s32[320,1]{1,0:T(8,128)} %broadcast_in_dim.26.source, bf16[128,64]{1,0:T(8,128)(2,1)} %pad.9.w_mix, bf16[16,256]{1,0:T(8,128)(2,1)} %interp.1, bf16[576,64]{1,0:T(8,128)(2,1)} %bitcast.17, f32[64,1]{1,0:T(8,128)} %copy.17.bias, ...), custom_call_target="tpu_custom_call" | custom-call | tf_op jit(solution)/shard_map/convolve/pallas_call | solution.py:245
  (10 shorter events, 0.1 us)
Async XLA Ops:
  0.0 12.1 %copy-start = (bf16[960,1104]{1,0:T(8,128)(2,1)S(1)}, bf16[960,1104]{1,0:T(8,128)(2,1)}, u32[]{:S(2)}) copy-start(bf16[960,1104]{1,0:T(8,128)(2,1)} %param.7) | copy-start | bytes 6359044
where the time goes:
time: 72.1 us; the launch traced here: 71.7 us
  Pallas kernels  56.8 us (79%)
  local copies, waits for them, and re-layouts  10.8 us (15%)
  between operations  3.42 us (5%)
    pallas_call x1, Pallas kernels, all_to_all(): pl.pallas_call(functools.partial(exchange, n_dev, n_lon), out_shape=jax.S...  36.2 us
    pallas_call x1, Pallas kernels, per_device(): pl.pallas_call(convolve, grid=(STEPS,), out_shape=jax.ShapeDtypeStruct((c...  20.6 us
    gather x1, local copies, waits for them, and re-layouts, per_device(): outgoing = coarse[jnp.clip(table, 0, held - 1).reshape(-1)]  2.83 us
    unnamed x4, local copies, waits for them, and re-layouts  1.67 us
    slice x1, local copies, waits for them, and re-layouts, per_device(): first = block_ids[0, 0]  1.45 us

commit v1 on v0

--- a/solution.py
+++ b/solution.py
@@ -19,15 +19,15 @@
     def copy(d):
         target = lax.rem(me + d, n_dev)
         return pltpu.make_async_remote_copy(
-            src_ref=out_ref.at[target],
-            dst_ref=in_ref.at[me],
+            src_ref=out_ref.at[:, target],
+            dst_ref=in_ref.at[:, me],
             send_sem=send_sem.at[d],
             recv_sem=recv_sem.at[d],
             device_id={"lat": target // n_lon, "lon": lax.rem(target, n_lon)},
             device_id_type=pl.DeviceIdType.MESH,
         )
 
-    own = pltpu.make_async_copy(out_ref.at[me], in_ref.at[me], own_sem)
+    own = pltpu.make_async_copy(out_ref.at[:, me], in_ref.at[:, me], own_sem)
 
     @pl.loop(1, n_dev)
     def _(d):
@@ -60,6 +60,45 @@
 
 
 NT = (((1,), (1,)), ((), ()))
+
+
+def offsets(ids, held, n_lat, n_lon):
+    first = ids[0, 0]
+    cols = ids[0, n_lat * PC] - first
+    holder = lax.div(first, held)
+    spot = first - holder * held
+    down = lax.div(spot, cols)
+    r0 = down * n_lat + lax.div(holder, n_lon)
+    c0 = (spot - down * cols) * n_lon + lax.rem(holder, n_lon)
+    return r0, c0, cols
+
+
+def pack(n_lat, n_lon, per_col, ids, coarse, w_mix, out, cells):
+    f32, bf16 = jnp.float32, jnp.bfloat16
+    n_dev = n_lat * n_lon
+    held, width = coarse.shape
+    c_in, c_out = width // SIDE, w_mix.shape[1]
+    r0, c0, cols = offsets(ids, held, n_lat, n_lon)
+    lat, lon = lax.axis_index("lat"), lax.axis_index("lon")
+    count = out.shape[0]
+    index = lax.broadcasted_iota(jnp.int32, (count, 1), 0)
+    tile, place = index % n_dev, index // n_dev
+    row_from = r0 + (tile // n_lon) * PR - 1 + n_lat
+    col_from = c0 + (tile % n_lon) * PC
+    row = row_from + (lat - row_from) % n_lat + (place // per_col) * n_lat
+    col = col_from + (lon - col_from) % n_lon + (place % per_col) * n_lon
+    col = jnp.where(col >= cols * n_lon, col - cols * n_lon, col)
+    table = jnp.clip((row // n_lat - 1) * cols + col // n_lon, 0, held - 1)
+    pick = lax.broadcasted_iota(jnp.int32, (count, held), 1) == table
+    picked = jnp.dot(pick.astype(f32).astype(bf16), coarse[...], preferred_element_type=f32)
+    mixer = w_mix[...]
+    for k in range(0, SIDE, 2):
+        pair = [
+            jnp.dot(picked[:, q * c_in:(q + 1) * c_in].astype(bf16), mixer, preferred_element_type=f32)
+            for q in (k, k + 1)
+        ]
+        cells[:, k // 2, :] = jnp.concatenate(pair, axis=1)
+    out[...] = cells[...].astype(bf16)
 
 
 def build_maps(interp, rhs, up, down):
@@ -123,26 +162,64 @@
         rhs[pair, 9 * rows:, at:at + breadth] = total.astype(bf16)
 
 
-def build_left(arrived, source, w_mix, kernel, grouped, left):
+def build_left(n_lat, n_lon, per_col, held, ids, valid, arrived, edges, kernel, grouped, left, land, cells):
     f32, bf16 = jnp.float32, jnp.bfloat16
+    n_dev = n_lat * n_lon
     rows = SIDE * PC
     high = PR + 2
-    c_in = arrived.shape[1] // SIDE
+    main = high * PC
     c_out = kernel.shape[0] // 9
-    slots = lax.broadcasted_iota(jnp.int32, (source.shape[0], arrived.shape[0]), 1)
-    pick = (slots == source[...]).astype(f32).astype(bf16)
-    window = jnp.dot(pick, arrived[...], preferred_element_type=f32)
-    grouped[...] = jnp.zeros_like(grouped)
-    for k in range(SIDE):
-        cell = window[:, k * c_in:(k + 1) * c_in]
-        grouped[:, 0, k, :, :c_in] = cell[:high * PC].reshape(high, PC, c_in)
-        grouped[:, 1, k, :, :c_in] = cell[high * PC:].reshape(high, PC, c_in)
-    both = lax.dot_general(kernel[...], w_mix[...], NT, preferred_element_type=f32).astype(bf16)
+    r0, c0, _ = offsets(ids, held, n_lat, n_lon)
+    lat, lon = lax.axis_index("lat"), lax.axis_index("lon")
+    index = lax.broadcasted_iota(jnp.int32, (2 * main, 1), 0)
+    inner = index < main
+    at = jnp.where(inner, index, index - main)
+    wr = at // PC
+    pc = at % PC
+    side = pc // 4
+    owner = (r0 + lat * PR - 1 + n_lat + wr) % n_lat * n_lon + (c0 + lon * PC + pc) % n_lon
+    rank = wr // n_lat * per_col + pc // n_lon
+    source = jnp.where(inner, rank * n_dev + owner, arrived.shape[0] + side * high + wr)
+    tile_lat = lat + (wr == high - 1).astype(jnp.int32) - (wr == 0).astype(jnp.int32)
+    tile_lon = lon + jnp.where(inner, 0, 2 * side - 1)
+    slot_row = jnp.where(wr == 0, PR - 1, jnp.where(wr == high - 1, 0, wr - 1))
+    slot = slot_row * PC + jnp.where(inner, pc, jnp.where(side == 0, PC - 1, 0))
+    inside = (tile_lat >= 0) & (tile_lat < n_lat) & (tile_lon >= 0) & (tile_lon < n_lon)
+    tile = jnp.where(inside, tile_lat * n_lon + tile_lon, -1)
+    alive = (valid[...] > 0).astype(f32)
+    whose = lax.broadcasted_iota(jnp.int32, (2 * main, n_dev), 1) == tile
+    seen = jnp.dot(whose.astype(f32).astype(bf16), alive.astype(bf16), preferred_element_type=f32)
+    spot = lax.broadcasted_iota(jnp.int32, (2 * main, PR * PC), 1) == slot
+    live = jnp.sum(jnp.where(spot, seen, 0.0), axis=1, keepdims=True)
+    source = jnp.where(live > 0, source, -1)
+
+    mine = (valid[pl.ds(lat * n_lon + lon, 1), :] > 0).astype(f32)
+    of_row = lax.broadcasted_iota(jnp.int32, (PR, PR * PC), 0)
+    of_slot = lax.broadcasted_iota(jnp.int32, (PR, PR * PC), 1)
+    by_row = jnp.where(of_slot // PC == of_row, mine, 0.0).astype(bf16)
+    from_slot = lax.broadcasted_iota(jnp.int32, (PR * PC, rows), 0)
+    to_lane = lax.broadcasted_iota(jnp.int32, (PR * PC, rows), 1)
+    widen = (from_slot % PC == to_lane // SIDE).astype(f32).astype(bf16)
+    mask = jnp.dot(by_row, widen, preferred_element_type=f32)
+    for step in range(STEPS):
+        land[step] = mask[step * (PR // STEPS):(step + 1) * (PR // STEPS)]
+
+    cells[:arrived.shape[0]] = arrived[...].astype(f32)
+    cells[arrived.shape[0]:] = edges[...].astype(f32)
+    slots = lax.broadcasted_iota(jnp.int32, (2 * main, cells.shape[0]), 1)
+    pick = (slots == source).astype(f32).astype(bf16)
+    for k in range(0, SIDE, 2):
+        pair = jnp.dot(pick, cells[:, k // 2, :].astype(bf16), preferred_element_type=f32)
+        for q in (0, 1):
+            cell = pair[:, q * c_out:(q + 1) * c_out]
+            grouped[:, 0, k + q] = cell[:main].reshape(high, PC, c_out)
+            grouped[:, 1, k + q] = cell[main:].reshape(high, PC, c_out)
+    both = kernel[...]
     lane = lax.broadcasted_iota(jnp.int32, (c_out, rows), 1) % PC
 
     @pl.loop(0, high)
     def _(wr):
-        cells = grouped[wr].reshape(2 * rows, 128).astype(bf16)
+        cells = grouped[wr].reshape(2 * rows, c_out).astype(bf16)
         res = lax.dot_general(both, cells, NT, preferred_element_type=f32)
         at = pl.ds(pl.multiple_of(wr * c_out, c_out), c_out)
         edge = jnp.zeros((c_out, rows), f32)
@@ -155,7 +232,7 @@
         left[at, 9 * rows:] = edge.astype(bf16)
 
 
-def convolve(arrived, source, w_mix, interp, kernel, bias, land, out, grouped, left, rhs, up, down, fine):
+def convolve(n_lat, n_lon, per_col, held, ids, valid, arrived, edges, interp, kernel, bias, out, grouped, left, rhs, up, down, fine, land, cells):
     f32 = jnp.float32
     rows = SIDE * PC
     c_out = kernel.shape[0] // 9
@@ -166,7 +243,7 @@
     @pl.when(step == 0)
     def _():
         build_maps(interp[...], rhs, up, down)
-        build_left(arrived, source, w_mix, kernel, grouped, left)
+        build_left(n_lat, n_lon, per_col, held, ids, valid, arrived, edges, kernel, grouped, left, land, cells)
 
     base = pl.multiple_of(step * many, c_out)
     above = pl.ds(base, many)
@@ -203,65 +280,66 @@
     lat, lon = lax.axis_index("lat"), lax.axis_index("lon")
     held = coarse.shape[0]
     channels = w_mix.shape[1]
-    high, wide = PR + 2, PC + 2
-    per_col = -(-wide // n_lon)
-    most = -(-(-(-high // n_lat) * per_col) // 16) * 16
+    high = PR + 2
+    per_col = -(-PC // n_lon)
+    most = -(-high // n_lat) * per_col
+    count = n_dev * most
+    lanes = 2 * channels
+    cell = (SIDE // 2, lanes)
     i32 = jnp.int32
-    first = block_ids[0, 0]
-    cols = block_ids[0, n_lat * PC] - first
-    spot, holder = first % held, first // held
-    r0 = (spot // cols) * n_lat + holder // n_lon
-    c0 = (spot % cols) * n_lon + holder % n_lon
-
-    tile = jnp.arange(n_dev, dtype=i32)[:, None]
-    place = jnp.arange(most, dtype=i32)[None, :]
-    row_from = r0 + (tile // n_lon) * PR - 1
-    col_from = c0 + (tile % n_lon) * PC - 1
-    row = row_from + jnp.mod(lat - row_from, n_lat) + (place // per_col) * n_lat
-    col = col_from + jnp.mod(lon - col_from, n_lon) + (place % per_col) * n_lon
-    table = jnp.floor_divide(row, n_lat) * cols + jnp.mod(col, cols * n_lon) // n_lon
-    outgoing = coarse[jnp.clip(table, 0, held - 1).reshape(-1)]
-    arrived = all_to_all(outgoing.reshape(n_dev, most, coarse.shape[1]), n_lat, n_lon)
-
-    image = valid.reshape(n_lat, n_lon, PR, PC).transpose(0, 2, 1, 3)
-    image = jnp.pad(image.reshape(n_lat * PR, n_lon * PC), 1)
-    live = lax.dynamic_slice(image, (lat * PR, lon * PC), (high, wide))
-    wr = jnp.arange(high, dtype=i32)[:, None]
-    wc = jnp.arange(wide, dtype=i32)[None, :]
-    owner = jnp.mod(r0 + lat * PR - 1 + wr, n_lat) * n_lon
-    owner = owner + jnp.mod(c0 + lon * PC - 1 + wc, n_lon)
-    rank = (wr // n_lat) * per_col + wc // n_lon
-    source = jnp.where(live > 0, owner * most + rank, -1)
-    edges = jnp.repeat(source[:, ::wide - 1], 4, axis=1)
-    source = jnp.concatenate([source[:, 1:-1].reshape(-1), edges.reshape(-1)])[:, None]
-    land = jnp.repeat(live[1:-1, 1:-1].astype(jnp.float32), SIDE, axis=1)
+    vmem = pl.BlockSpec(memory_space=pltpu.VMEM)
+    smem = pl.BlockSpec(memory_space=pltpu.SMEM)
+    outgoing = pl.pallas_call(
+        functools.partial(pack, n_lat, n_lon, per_col),
+        out_shape=jax.ShapeDtypeStruct((count,) + cell, jnp.bfloat16),
+        in_specs=[smem, vmem, vmem],
+        out_specs=vmem,
+        scratch_shapes=[pltpu.VMEM((count,) + cell, jnp.float32)],
+        compiler_params=pltpu.CompilerParams(vmem_limit_bytes=40 * 1024 * 1024),
+        name="pack",
+    )(block_ids[:1], coarse, w_mix)
+    arrived = all_to_all(outgoing.reshape((most, n_dev) + cell), n_lat, n_lon)
+    arrived = arrived.reshape((count,) + cell)
+
+    first = block_ids[0, 0] // held
+    wr = jnp.arange(high, dtype=i32)[None, :]
+    pc = jnp.array([[PC - 1], [0]], i32)
+    owner = jnp.mod(first // n_lon + lat * PR - 1 + wr, n_lat) * n_lon
+    owner = owner + jnp.mod(first % n_lon + lon * PC + pc, n_lon)
+    rank = wr // n_lat * per_col + pc // n_lon
+    ends = arrived[rank * n_dev + owner]
+    ahead = [(i, i + 1) for i in range(n_lon - 1)]
+    back = [(i + 1, i) for i in range(n_lon - 1)]
+    edges = jnp.concatenate(
+        [lax.ppermute(ends[0], "lon", ahead), lax.ppermute(ends[1], "lon", back)], axis=0
+    )
 
     rows = SIDE * PC
     full = lambda *shape: pl.BlockSpec(shape, lambda i: (0,) * len(shape))
-    arrived = arrived.reshape(n_dev * most, coarse.shape[1])
-    count = PR // STEPS
+    part = PR // STEPS
     taps = kernel.reshape(9 * channels, channels)
-    mixer = jnp.pad(w_mix, ((0, 128 - w_mix.shape[0]), (0, 0)))
     return pl.pallas_call(
-        convolve,
+        functools.partial(convolve, n_lat, n_lon, per_col, held),
         grid=(STEPS,),
         out_shape=jax.ShapeDtypeStruct((channels, PR * SIDE, rows), jnp.bfloat16),
         in_specs=[
-            full(*arrived.shape), full(*source.shape), full(*mixer.shape), full(*interp.shape),
-            full(*taps.shape), full(channels, 1), full(STEPS, count, rows),
+            smem, full(*valid.shape), full(*arrived.shape), full(*edges.shape),
+            full(*interp.shape), full(*taps.shape), full(channels, 1),
         ],
-        out_specs=pl.BlockSpec((channels, count * SIDE, rows), lambda i: (0, i, 0)),
+        out_specs=pl.BlockSpec((channels, part * SIDE, rows), lambda i: (0, i, 0)),
         scratch_shapes=[
-            pltpu.VMEM((high, 2, SIDE, PC, 128), jnp.float32),
+            pltpu.VMEM((high, 2, SIDE, PC, channels), jnp.float32),
             pltpu.VMEM((high * channels, 10 * rows), jnp.bfloat16),
             pltpu.VMEM((SIDE // 2, 10 * rows, 2 * rows), jnp.bfloat16),
             pltpu.VMEM((4 * rows, 2 * rows), jnp.bfloat16),
             pltpu.VMEM((4 * rows, 2 * rows), jnp.bfloat16),
-            pltpu.VMEM((count * channels * SIDE, rows), jnp.float32),
+            pltpu.VMEM((part * channels * SIDE, rows), jnp.float32),
+            pltpu.VMEM((STEPS, part, rows), jnp.float32),
+            pltpu.VMEM((count + 2 * high,) + cell, jnp.float32),
         ],
         compiler_params=pltpu.CompilerParams(vmem_limit_bytes=60 * 1024 * 1024),
         name="convolve",
-    )(arrived, source, mixer, interp, taps, bias[:, None], land.reshape(STEPS, count, rows))
+    )(block_ids[:1], valid, arrived, edges, interp, taps, bias[:, None])
 
 
 def solution(mesh):

time: 72.1 us -> 60.1 us (0.83)
  Pallas kernels: 56.8 us -> 41.1 us
  starting transfers between devices: 0 us -> 3.87 us
  waiting for transfers between devices: 0 us -> 3.25 us
  local copies, waits for them, and re-layouts: 10.8 us -> 8.07 us
  between operations: 3.42 us -> 2.05 us
    pallas_call x1, Pallas kernels: 36.2 us -> 19.4 us  [all_to_all(): pl.pallas_call(functools.partial(exchange, n_dev, n_lon), out_shape=jax.S...]
    ppermute x0 -> x2, starting transfers between devices: none -> 3.87 us  [the longest x1 2.58 us: per_device(): lax.ppermute(ends[0], 'lon', ahead)]
    ppermute x0 -> x2, waiting for transfers between devices: none -> 3.25 us  [the longest x1 3.24 us: per_device(): lax.ppermute(ends[1], 'lon', back)]
    unnamed x4 -> x7, local copies, waits for them, and re-layouts: 1.67 us -> 3.16 us
    gather x1, local copies, waits for them, and re-layouts: 2.83 us -> 1.57 us  [per_device(): ends = arrived[rank * n_dev + owner]]
    pallas_call x1 -> x2, Pallas kernels: 20.6 us -> 21.7 us  [the longest x1 19.8 us: per_device(): pl.pallas_call(functools.partial(convolve, n_lat, n_lon, per_col, held),...]
    broadcast_in_dim x3 -> x0, local copies, waits for them, and re-layouts: 0.91 us -> none  [the longest x1 0.76 us: per_device(): jnp.concatenate([source[:, 1:-1].reshape(-1), edges.reshape(-1)])[:, None]]
    another operation x2 -> x0, local copies, waits for them, and re-layouts: 0.81 us -> none  [the longest x1 0.7 us: per_device(): land.reshape(STEPS, count, rows)]
  transfers between devices with their start and end apart: 0 -> 2, of which waited for: 0 -> 1; matrix products, arithmetic and copies ran while one was open for 0% -> 2% of each run, Pallas kernels for 0% -> 0%
where the time goes in v1:
time: 60.1 us; the launch traced here: 59.7 us
  Pallas kernels  41.1 us (68%)
  local copies, waits for them, and re-layouts  8.07 us (13%)
  starting transfers between devices  3.87 us (6%)
  waiting for transfers between devices  3.25 us (5%)
  between operations  2.05 us (3%)
  other arithmetic  1.4 us (2%)
    pallas_call x1, Pallas kernels, per_device(): pl.pallas_call(functools.partial(convolve, n_lat, n_lon, per_col, held),...  19.8 us
    pallas_call x1, Pallas kernels, all_to_all(): pl.pallas_call(functools.partial(exchange, n_dev, n_lon), out_shape=jax.S...  19.4 us
    ppermute x1, waiting for transfers between devices, per_device(): lax.ppermute(ends[1], 'lon', back)  3.24 us
    unnamed x7, local copies, waits for them, and re-layouts  3.16 us
    ppermute x1, starting transfers between devices, per_device(): lax.ppermute(ends[0], 'lon', ahead)  2.58 us
    pallas_call x1, Pallas kernels, per_device(): pl.pallas_call(functools.partial(pack, n_lat, n_lon, per_col), out_shape=...  1.84 us
    gather x1, local copies, waits for them, and re-layouts, per_device(): ends = arrived[rank * n_dev + owner]  1.57 us
    broadcast_in_dim x1, local copies, waits for them, and re-layouts, per_device(): bias[:, None]  1.35 us
  transfers between devices with their start and end apart: 2, of which 1 were waited for; matrix products, arithmetic and copies ran while one was open for 2% of the time, Pallas kernels for 0%

profile of v1, /device:TPU:0, one launch (start us, length us, event | category | flops | bytes accessed | tf_op | source)
XLA Modules:
  0.0 59.7 jit_solution(5819102839922321106)
XLA Ops:
  0.0 1.2 %slice.14 = s32[1,1]{1,0:T(1,128)} slice(s32[32,144]{1,0:T(8,128)} %param.13), slice={[0:1], [0:1]} | slice | bytes 8 | tf_op jit(solution)/shard_map/slice | solution.py:304
  3.2 0.7 %slice.13.ids = s32[1,144]{1,0:T(1,128)S(1)} slice(s32[32,144]{1,0:T(8,128)} %param.13), slice={[0:1], [0:144]} | slice | bytes 1152 | tf_op jit(solution)/shard_map/slice | solution.py:342
  3.9 0.0 copy-start.2
  3.9 0.7 %fusion.1 = s32[2]{0:T(128)S(1)} fusion(s32[2,1]{0,1:T(1,128)} %constant.101.clone, s32[]{:T(128)S(6)} %add.131), kind=kLoop, calls=%fused_computation.15 | loop fusion | flops 24 | bytes 20 | tf_op jit(solution)/shard_map/add | solution.py:308
  4.6 0.1 compare_select_fusion
  4.6 0.1 reshape.192
  4.7 0.8 %copy.9.w_mix = bf16[69,64]{1,0:T(8,128)(2,1)S(1)} copy(bf16[69,64]{0,1:T(8,128)(2,1)} %param.9) | data formatting | bytes 17664 | tf_op args[1]
  5.6 0.0 copy-start
  5.6 1.6 %copy-done = bf16[960,1104]{1,0:T(8,128)(2,1)S(1)} copy-done((bf16[960,1104]{1,0:T(8,128)(2,1)S(1)}, bf16[960,1104]{1,0:T(8,128)(2,1)}, u32[]{:S(2)}) %copy-start) | copy-done | bytes 2119704
  7.2 1.8 %pack.1 = bf16[160,8,128]{2,1,0:T(8,128)(2,1)S(1)} custom-call(s32[1,144]{1,0:T(1,128)S(1)} %slice.13.ids, bf16[960,1104]{1,0:T(8,128)(2,1)S(1)} %copy-done, bf16[69,64]{1,0:T(8,128)(2,1)S(1)} %copy.9.w_mix), custom_call_target="tpu_custom_call" | custom-call | tf_op jit(solution)/shard_map/pack/pallas_call | solution.py:292
  9.0 0.0 copy-start.1
  9.1 0.7 %copy-done.1 = bf16[160,8,128]{2,1,0:T(8,128)(2,1)} copy-done((bf16[160,8,128]{2,1,0:T(8,128)(2,1)}, bf16[160,8,128]{2,1,0:T(8,128)(2,1)S(1)}, u32[]{:S(2)}) %copy-start.1) | copy-done | bytes 327704
  9.8 19.4 %exchange.1 = bf16[5,32,8,128]{3,2,1,0:T(8,128)(2,1)} custom-call(bf16[5,32,8,128]{3,2,1,0:T(8,128)(2,1)} %bitcast.10), custom_call_target="tpu_custom_call" | custom-call | tf_op jit(solution)/shard_map/exchange/pallas_call | solution.py:47
  29.1 1.6 %gather_fusion = bf16[40,8,128]{2,1,0:T(8,128)(2,1)S(1)} fusion(bf16[160,8,128]{2,1,0:T(8,128)(2,1)} %bitcast.11, s32[1024]{0:T(1024)S(1)} %pad_clamp_fusion), kind=kCustom, calls=%fused_computation | custom fusion | bytes 164000 | tf_op jit(solution)/shard_map/gather | solution.py:310
  30.7 2.6 %collective-permute-start = (bf16[20,8,128]{2,1,0:T(8,128)(2,1)S(1)}, bf16[20,8,128]{2,1,0:T(8,128)(2,1)S(1)}, u32[]{:S(2)}, u32[]{:S(2)}) collective-permute-start(bf16[20,8,128]{2,1,0:T(8,128)(2,1)S(1)} %get-tuple-element.5), channel_id=1, source_target_pairs={{0,1},{1,2},{2,3},{3,4},{4,5},{5,6},{6,7},{8,9},{9,10},{10,11},{11... | collective-permute-start | bytes 122888 | tf_op jit(solution)/shard_map/ppermute | solution.py:314
  33.3 1.3 %collective-permute-start.1 = (bf16[20,8,128]{2,1,0:T(8,128)(2,1)S(1)}, bf16[20,8,128]{2,1,0:T(8,128)(2,1)S(1)}, u32[]{:S(2)}, u32[]{:S(2)}) collective-permute-start(bf16[20,8,128]{2,1,0:T(8,128)(2,1)S(1)} %get-tuple-element.6), channel_id=1, source_target_pairs={{1,0},{2,1},{3,2},{4,3},{5,4},{6,5},{7,6},{9,8},{10,9},{11,10},{12... | collective-permute-start | bytes 122888 | tf_op jit(solution)/shard_map/ppermute | solution.py:314
  34.6 1.3 %copy.10.bias = f32[64,1]{1,0:T(8,128)} copy(f32[64,1]{0,1:T(1,128)} %bitcast.14) | data formatting | bytes 512 | tf_op jit(solution)/shard_map/broadcast_in_dim | solution.py:342
  36.0 0.0 collective-permute-done
  36.0 3.2 %collective-permute-done.1 = bf16[20,8,128]{2,1,0:T(8,128)(2,1)S(1)} collective-permute-done((bf16[20,8,128]{2,1,0:T(8,128)(2,1)S(1)}, bf16[20,8,128]{2,1,0:T(8,128)(2,1)S(1)}, u32[]{:S(2)}, u32[]{:S(2)}) %collective-permute-start.1) | collective-permute-done | bytes 40992 | tf_op jit(solution)/shard_map/ppermute | solution.py:314
  39.2 0.6 %pad_maximum_fusion.edges = bf16[40,8,128]{2,1,0:T(8,128)(2,1)} fusion(bf16[20,8,128]{2,1,0:T(8,128)(2,1)S(1)} %collective-permute-done.1, bf16[20,8,128]{2,1,0:T(8,128)(2,1)S(1)} %collective-permute-done), kind=kLoop, calls=%fused_computation.1 | loop fusion | flops 40960 | bytes 163840 | tf_op jit(solution)/shard_map/concatenate | solution.py:313
  39.8 0.0 copy-done.2
  39.9 19.8 %convolve.1 = bf16[64,288,128]{2,1,0:T(8,128)(2,1)} custom-call(s32[1,144]{1,0:T(1,128)} %copy-done.2, s32[32,144]{1,0:T(8,128)} %valid.1, bf16[160,8,128]{2,1,0:T(8,128)(2,1)} %bitcast.12, bf16[40,8,128]{2,1,0:T(8,128)(2,1)} %pad_maximum_fusion.edges, bf16[16,256]{1,0:T(8,128)(2,1)} %interp.1, bf16[576,64]{1,0:T(8,128)(2,1)} %bitcast.13, f32[64,1]{1,0:T(8,128)} %copy.10.bias), custom_call_target="tpu_custom_call" | custom-call | tf_op jit(solution)/shard_map/convolve/pallas_call | solution.py:321
  (3 shorter events, 0.0 us)
Async XLA Ops:
  3.9 36.0 %copy-start.2 = (s32[1,144]{1,0:T(1,128)}, s32[1,144]{1,0:T(1,128)S(1)}, u32[]{:S(2)}) copy-start(s32[1,144]{1,0:T(1,128)S(1)} %slice.13.ids) | copy-start | bytes 1732
  5.6 1.6 %copy-start = (bf16[960,1104]{1,0:T(8,128)(2,1)S(1)}, bf16[960,1104]{1,0:T(8,128)(2,1)}, u32[]{:S(2)}) copy-start(bf16[960,1104]{1,0:T(8,128)(2,1)} %coarse.1) | copy-start | bytes 6359044
  9.0 0.7 %copy-start.1 = (bf16[160,8,128]{2,1,0:T(8,128)(2,1)}, bf16[160,8,128]{2,1,0:T(8,128)(2,1)S(1)}, u32[]{:S(2)}) copy-start(bf16[160,8,128]{2,1,0:T(8,128)(2,1)S(1)} %pack.1) | copy-start | bytes 983044
  30.7 5.2 %collective-permute-start = (bf16[20,8,128]{2,1,0:T(8,128)(2,1)S(1)}, bf16[20,8,128]{2,1,0:T(8,128)(2,1)S(1)}, u32[]{:S(2)}, u32[]{:S(2)}) collective-permute-start(bf16[20,8,128]{2,1,0:T(8,128)(2,1)S(1)} %get-tuple-element.5), channel_id=1, source_target_pairs={{0,1},{1,2},{2,3},{3,4},{4,5},{5,6},{6,7},{8,9},{9,10},{10,11},{11... | collective-permute-start | bytes 122888 | tf_op jit(solution)/shard_map/ppermute | solution.py:314
  33.3 5.9 %collective-permute-start.1 = (bf16[20,8,128]{2,1,0:T(8,128)(2,1)S(1)}, bf16[20,8,128]{2,1,0:T(8,128)(2,1)S(1)}, u32[]{:S(2)}, u32[]{:S(2)}) collective-permute-start(bf16[20,8,128]{2,1,0:T(8,128)(2,1)S(1)} %get-tuple-element.6), channel_id=1, source_target_pairs={{1,0},{2,1},{3,2},{4,3},{5,4},{6,5},{7,6},{9,8},{10,9},{11,10},{12... | collective-permute-start | bytes 122888 | tf_op jit(solution)/shard_map/ppermute | solution.py:314

commit v2 on v1

--- a/solution.py
+++ b/solution.py
@@ -19,15 +19,15 @@
     def copy(d):
         target = lax.rem(me + d, n_dev)
         return pltpu.make_async_remote_copy(
-            src_ref=out_ref.at[:, target],
-            dst_ref=in_ref.at[:, me],
+            src_ref=out_ref.at[target],
+            dst_ref=in_ref.at[me],
             send_sem=send_sem.at[d],
             recv_sem=recv_sem.at[d],
             device_id={"lat": target // n_lon, "lon": lax.rem(target, n_lon)},
             device_id_type=pl.DeviceIdType.MESH,
         )
 
-    own = pltpu.make_async_copy(out_ref.at[:, me], in_ref.at[:, me], own_sem)
+    own = pltpu.make_async_copy(out_ref.at[me], in_ref.at[me], own_sem)
 
     @pl.loop(1, n_dev)
     def _(d):
@@ -47,8 +47,8 @@
     return pl.pallas_call(
         functools.partial(exchange, n_dev, n_lon),
         out_shape=jax.ShapeDtypeStruct(outgoing.shape, outgoing.dtype),
-        in_specs=[pl.BlockSpec(memory_space=pl.ANY)],
-        out_specs=pl.BlockSpec(memory_space=pl.ANY),
+        in_specs=[pl.BlockSpec(memory_space=pltpu.VMEM)],
+        out_specs=pl.BlockSpec(memory_space=pltpu.VMEM),
         scratch_shapes=[
             pltpu.SemaphoreType.DMA((n_dev,)),
             pltpu.SemaphoreType.DMA((n_dev,)),
@@ -82,7 +82,10 @@
     lat, lon = lax.axis_index("lat"), lax.axis_index("lon")
     count = out.shape[0]
     index = lax.broadcasted_iota(jnp.int32, (count, 1), 0)
-    tile, place = index % n_dev, index // n_dev
+    most = count // n_dev
+    passed = index >= (lax.broadcasted_iota(jnp.int32, (count, n_dev), 1) + 1) * most
+    tile = jnp.sum(passed.astype(f32), axis=1, keepdims=True).astype(jnp.int32)
+    place = index - tile * most
     row_from = r0 + (tile // n_lon) * PR - 1 + n_lat
     col_from = c0 + (tile % n_lon) * PC
     row = row_from + (lat - row_from) % n_lat + (place // per_col) * n_lat
@@ -162,6 +165,27 @@
         rhs[pair, 9 * rows:, at:at + breadth] = total.astype(bf16)
 
 
+def choose_ends(n_lat, n_lon, per_col, held, ids, arrived, out, cells, chosen):
+    f32, bf16 = jnp.float32, jnp.bfloat16
+    r0, c0, _ = offsets(ids, held, n_lat, n_lon)
+    lat, lon = lax.axis_index("lat"), lax.axis_index("lon")
+    most = arrived.shape[0] // (n_lat * n_lon)
+    count = out.shape[0]
+    index = lax.broadcasted_iota(jnp.int32, (count, 1), 0)
+    low = index < count // 2
+    wr = jnp.where(low, index, index - count // 2)
+    pc = jnp.where(low, PC - 1, 0)
+    owner = (r0 + lat * PR - 1 + n_lat + wr) % n_lat * n_lon + (c0 + lon * PC + pc) % n_lon
+    source = owner * most + wr // n_lat * per_col + pc // n_lon
+    slots = lax.broadcasted_iota(jnp.int32, (count, arrived.shape[0]), 1)
+    pick = (slots == source).astype(f32).astype(bf16)
+    cells[...] = arrived[...].astype(f32)
+    for j in range(SIDE // 2):
+        block = cells[:, j, :].astype(bf16)
+        chosen[:, j, :] = jnp.dot(pick, block, preferred_element_type=f32)
+    out[...] = chosen[...].astype(bf16)
+
+
 def build_left(n_lat, n_lon, per_col, held, ids, valid, arrived, edges, kernel, grouped, left, land, cells):
     f32, bf16 = jnp.float32, jnp.bfloat16
     n_dev = n_lat * n_lon
@@ -179,7 +203,7 @@
     side = pc // 4
     owner = (r0 + lat * PR - 1 + n_lat + wr) % n_lat * n_lon + (c0 + lon * PC + pc) % n_lon
     rank = wr // n_lat * per_col + pc // n_lon
-    source = jnp.where(inner, rank * n_dev + owner, arrived.shape[0] + side * high + wr)
+    source = jnp.where(inner, owner * (arrived.shape[0] // n_dev) + rank, arrived.shape[0] + side * high + wr)
     tile_lat = lat + (wr == high - 1).astype(jnp.int32) - (wr == 0).astype(jnp.int32)
     tile_lon = lon + jnp.where(inner, 0, 2 * side - 1)
     slot_row = jnp.where(wr == 0, PR - 1, jnp.where(wr == high - 1, 0, wr - 1))
@@ -251,11 +275,14 @@
     below = pl.ds(pl.multiple_of(base + 2 * c_out, c_out), many)
     mask = land[step]
     pairs = SIDE // 2
+    diagonal = lax.broadcasted_iota(jnp.int32, (c_out, c_out), 0)
+    diagonal = diagonal == lax.broadcasted_iota(jnp.int32, (c_out, c_out), 1)
+    shift = jnp.sum(jnp.where(diagonal, bias[...], 0.0), axis=1, keepdims=True)
 
     def put(total, fys):
         for half, fy in enumerate(fys):
             part = total[:, half * rows:(half + 1) * rows].reshape(count, c_out, rows)
-            part = (part + bias[...][None]) * mask[:, None, :]
+            part = (part + shift[None]) * mask[:, None, :]
             fine[pl.ds(fy, many, stride=SIDE), :] = part.reshape(many, rows)
 
     for pair in range(pairs):
@@ -277,7 +304,6 @@
     n_lat = lax.axis_size("lat")
     n_lon = lax.axis_size("lon")
     n_dev = n_lat * n_lon
-    lat, lon = lax.axis_index("lat"), lax.axis_index("lon")
     held = coarse.shape[0]
     channels = w_mix.shape[1]
     high = PR + 2
@@ -286,7 +312,6 @@
     count = n_dev * most
     lanes = 2 * channels
     cell = (SIDE // 2, lanes)
-    i32 = jnp.int32
     vmem = pl.BlockSpec(memory_space=pltpu.VMEM)
     smem = pl.BlockSpec(memory_space=pltpu.SMEM)
     outgoing = pl.pallas_call(
@@ -297,21 +322,25 @@
         scratch_shapes=[pltpu.VMEM((count,) + cell, jnp.float32)],
         compiler_params=pltpu.CompilerParams(vmem_limit_bytes=40 * 1024 * 1024),
         name="pack",
-    )(block_ids[:1], coarse, w_mix)
-    arrived = all_to_all(outgoing.reshape((most, n_dev) + cell), n_lat, n_lon)
+    )(block_ids, coarse, w_mix)
+    arrived = all_to_all(outgoing.reshape((n_dev, most) + cell), n_lat, n_lon)
     arrived = arrived.reshape((count,) + cell)
 
-    first = block_ids[0, 0] // held
-    wr = jnp.arange(high, dtype=i32)[None, :]
-    pc = jnp.array([[PC - 1], [0]], i32)
-    owner = jnp.mod(first // n_lon + lat * PR - 1 + wr, n_lat) * n_lon
-    owner = owner + jnp.mod(first % n_lon + lon * PC + pc, n_lon)
-    rank = wr // n_lat * per_col + pc // n_lon
-    ends = arrived[rank * n_dev + owner]
+    ends = pl.pallas_call(
+        functools.partial(choose_ends, n_lat, n_lon, per_col, held),
+        out_shape=jax.ShapeDtypeStruct((2 * high,) + cell, jnp.bfloat16),
+        in_specs=[smem, vmem],
+        out_specs=vmem,
+        scratch_shapes=[
+            pltpu.VMEM((count,) + cell, jnp.float32),
+            pltpu.VMEM((2 * high,) + cell, jnp.float32),
+        ],
+        name="choose_ends",
+    )(block_ids, arrived)
     ahead = [(i, i + 1) for i in range(n_lon - 1)]
     back = [(i + 1, i) for i in range(n_lon - 1)]
     edges = jnp.concatenate(
-        [lax.ppermute(ends[0], "lon", ahead), lax.ppermute(ends[1], "lon", back)], axis=0
+        [lax.ppermute(ends[:high], "lon", ahead), lax.ppermute(ends[high:], "lon", back)], axis=0
     )
 
     rows = SIDE * PC
@@ -324,7 +353,7 @@
         out_shape=jax.ShapeDtypeStruct((channels, PR * SIDE, rows), jnp.bfloat16),
         in_specs=[
             smem, full(*valid.shape), full(*arrived.shape), full(*edges.shape),
-            full(*interp.shape), full(*taps.shape), full(channels, 1),
+            full(*interp.shape), full(*taps.shape), full(1, channels),
         ],
         out_specs=pl.BlockSpec((channels, part * SIDE, rows), lambda i: (0, i, 0)),
         scratch_shapes=[
@@ -339,7 +368,7 @@
         ],
         compiler_params=pltpu.CompilerParams(vmem_limit_bytes=60 * 1024 * 1024),
         name="convolve",
-    )(block_ids[:1], valid, arrived, edges, interp, taps, bias[:, None])
+    )(block_ids, valid, arrived, edges, interp, taps, bias[None, :])
 
 
 def solution(mesh):

time: 60.1 us -> 60.3 us (level)
  Pallas kernels: 41.1 us -> 45.9 us
  local copies, waits for them, and re-layouts: 8.07 us -> 4.72 us
  between operations: 2.05 us -> 0.05 us
  waiting for transfers between devices: 3.25 us -> 4.6 us
  other arithmetic: 1.4 us -> 0.64 us
    pallas_call x0 -> x1, Pallas kernels: none -> 2.72 us  [per_device(): pl.pallas_call(functools.partial(choose_ends, n_lat, n_lon, per_col, held...]
    gather x1 -> x0, local copies, waits for them, and re-layouts: 1.57 us -> none  [per_device(): ends = arrived[rank * n_dev + owner]]
    pallas_call x1, Pallas kernels: 19.4 us -> 20.7 us  [all_to_all(): pl.pallas_call(functools.partial(exchange, n_dev, n_lon), out_shape=jax.S...]
    ppermute x2, waiting for transfers between devices: 3.25 us -> 4.6 us  [the longest x1 4.24 us: per_device(): lax.ppermute(ends[high:], 'lon', back)]
    broadcast_in_dim x1 -> x0, local copies, waits for them, and re-layouts: 1.35 us -> none  [per_device(): bias[:, None]]
    slice x3 -> x1, local copies, waits for them, and re-layouts: 1.9 us -> 0.8 us  [per_device(): ends[:high]]
    unnamed x7, local copies, waits for them, and re-layouts: 3.16 us -> 3.92 us
    add x1 -> x0, other arithmetic: 0.67 us -> none  [per_device(): owner = owner + jnp.mod(first % n_lon + lon * PC + pc, n_lon)]
  transfers between devices with their start and end apart: 2 -> 2, of which waited for: 1 -> 2; matrix products, arithmetic and copies ran while one was open for 2% -> 0% of each run, Pallas kernels for 0% -> 0%
where the time goes in v2:
time: 60.3 us; the launch traced here: 59.8 us
  Pallas kernels  45.9 us (76%)
  local copies, waits for them, and re-layouts  4.72 us (8%)
  waiting for transfers between devices  4.6 us (8%)
  starting transfers between devices  3.86 us (6%)
  other arithmetic  0.64 us (1%)
    pallas_call x1, Pallas kernels, all_to_all(): pl.pallas_call(functools.partial(exchange, n_dev, n_lon), out_shape=jax.S...  20.7 us
    pallas_call x1, Pallas kernels, per_device(): pl.pallas_call(functools.partial(convolve, n_lat, n_lon, per_col, held),...  20 us
    ppermute x1, waiting for transfers between devices, per_device(): lax.ppermute(ends[high:], 'lon', back)  4.24 us
    unnamed x7, local copies, waits for them, and re-layouts  3.92 us
    pallas_call x1, Pallas kernels, per_device(): pl.pallas_call(functools.partial(choose_ends, n_lat, n_lon, per_col, held...  2.72 us
    ppermute x1, starting transfers between devices, per_device(): lax.ppermute(ends[:high], 'lon', ahead)  2.56 us
    pallas_call x1, Pallas kernels, per_device(): pl.pallas_call(functools.partial(pack, n_lat, n_lon, per_col), out_shape=...  2.48 us
    ppermute x1, starting transfers between devices, per_device(): lax.ppermute(ends[high:], 'lon', back)  1.29 us
  transfers between devices with their start and end apart: 2, of which 2 were waited for; matrix products, arithmetic and copies ran while one was open for 0% of the time, Pallas kernels for 0%

profile of v2, /device:TPU:0, one launch (start us, length us, event | category | flops | bytes accessed | tf_op | source)
XLA Modules:
  0.0 59.8 jit_solution(12564854470404599900)
XLA Ops:
  0.0 0.8 %copy.8.w_mix = bf16[69,64]{1,0:T(8,128)(2,1)S(1)} copy(bf16[69,64]{0,1:T(8,128)(2,1)} %param.8) | data formatting | bytes 17664 | tf_op args[1]
  0.8 0.0 copy-start
  0.8 1.6 %copy-done = bf16[960,1104]{1,0:T(8,128)(2,1)S(1)} copy-done((bf16[960,1104]{1,0:T(8,128)(2,1)S(1)}, bf16[960,1104]{1,0:T(8,128)(2,1)}, u32[]{:S(2)}) %copy-start) | copy-done | bytes 2119704
  2.5 0.0 copy-start.2
  2.5 0.8 %copy-done.2 = s32[32,144]{1,0:T(8,128)S(1)} copy-done((s32[32,144]{1,0:T(8,128)S(1)}, s32[32,144]{1,0:T(8,128)}, u32[]{:S(2)}) %copy-start.2) | copy-done | bytes 18456
  3.2 2.5 %pack.1 = bf16[160,8,128]{2,1,0:T(8,128)(2,1)S(1)} custom-call(s32[32,144]{1,0:T(8,128)S(1)} %copy-done.2, bf16[960,1104]{1,0:T(8,128)(2,1)S(1)} %copy-done, bf16[69,64]{1,0:T(8,128)(2,1)S(1)} %copy.8.w_mix), custom_call_target="tpu_custom_call" | custom-call | tf_op jit(solution)/shard_map/pack/pallas_call | solution.py:317
  5.7 0.0 copy-start.1
  5.7 0.7 %copy-done.1 = bf16[160,8,128]{2,1,0:T(8,128)(2,1)} copy-done((bf16[160,8,128]{2,1,0:T(8,128)(2,1)}, bf16[160,8,128]{2,1,0:T(8,128)(2,1)S(1)}, u32[]{:S(2)}) %copy-start.1) | copy-done | bytes 327704
  6.4 20.7 %exchange.1 = bf16[32,5,8,128]{3,2,1,0:T(8,128)(2,1)} custom-call(bf16[32,5,8,128]{3,2,1,0:T(8,128)(2,1)} %bitcast.4), custom_call_target="tpu_custom_call" | custom-call | tf_op jit(solution)/shard_map/exchange/pallas_call | solution.py:47
  27.2 2.7 %choose_ends.1 = bf16[40,8,128]{2,1,0:T(8,128)(2,1)} custom-call(s32[32,144]{1,0:T(8,128)} %ids.5, bf16[160,8,128]{2,1,0:T(8,128)(2,1)} %bitcast.5), custom_call_target="tpu_custom_call" | custom-call | tf_op jit(solution)/shard_map/choose_ends/pallas_call | solution.py:329
  29.9 0.8 %fusion = (bf16[20,8,128]{2,1,0:T(8,128)(2,1)S(1)}, bf16[20,8,128]{2,1,0:T(8,128)(2,1)S(1)}) fusion(bf16[40,8,128]{2,1,0:T(8,128)(2,1)} %choose_ends.1), kind=kLoop, calls=%fused_computation.1 | loop fusion | bytes 163840 | tf_op jit(solution)/shard_map/slice | solution.py:343
  30.7 2.6 %collective-permute-start = (bf16[20,8,128]{2,1,0:T(8,128)(2,1)S(1)}, bf16[20,8,128]{2,1,0:T(8,128)(2,1)S(1)}, u32[]{:S(2)}, u32[]{:S(2)}) collective-permute-start(bf16[20,8,128]{2,1,0:T(8,128)(2,1)S(1)} %get-tuple-element.5), channel_id=1, source_target_pairs={{0,1},{1,2},{2,3},{3,4},{4,5},{5,6},{6,7},{8,9},{9,10},{10,11},{11... | collective-permute-start | bytes 122888 | tf_op jit(solution)/shard_map/ppermute | solution.py:343
  33.3 1.3 %collective-permute-start.1 = (bf16[20,8,128]{2,1,0:T(8,128)(2,1)S(1)}, bf16[20,8,128]{2,1,0:T(8,128)(2,1)S(1)}, u32[]{:S(2)}, u32[]{:S(2)}) collective-permute-start(bf16[20,8,128]{2,1,0:T(8,128)(2,1)S(1)} %get-tuple-element.6), channel_id=1, source_target_pairs={{1,0},{2,1},{3,2},{4,3},{5,4},{6,5},{7,6},{9,8},{10,9},{11,10},{12... | collective-permute-start | bytes 122888 | tf_op jit(solution)/shard_map/ppermute | solution.py:343
  34.6 0.4 collective-permute-done
  34.9 4.2 %collective-permute-done.1 = bf16[20,8,128]{2,1,0:T(8,128)(2,1)S(1)} collective-permute-done((bf16[20,8,128]{2,1,0:T(8,128)(2,1)S(1)}, bf16[20,8,128]{2,1,0:T(8,128)(2,1)S(1)}, u32[]{:S(2)}, u32[]{:S(2)}) %collective-permute-start.1) | collective-permute-done | bytes 40992 | tf_op jit(solution)/shard_map/ppermute | solution.py:343
  39.2 0.6 %pad_maximum_fusion.edges = bf16[40,8,128]{2,1,0:T(8,128)(2,1)} fusion(bf16[20,8,128]{2,1,0:T(8,128)(2,1)S(1)} %collective-permute-done.1, bf16[20,8,128]{2,1,0:T(8,128)(2,1)S(1)} %collective-permute-done), kind=kLoop, calls=%fused_computation | loop fusion | flops 40960 | bytes 163840 | tf_op jit(solution)/shard_map/concatenate | solution.py:342
  39.8 20.0 %convolve.1 = bf16[64,288,128]{2,1,0:T(8,128)(2,1)} custom-call(s32[32,144]{1,0:T(8,128)} %ids.5, s32[32,144]{1,0:T(8,128)} %valid.1, bf16[160,8,128]{2,1,0:T(8,128)(2,1)} %bitcast.6, bf16[40,8,128]{2,1,0:T(8,128)(2,1)} %pad_maximum_fusion.edges, bf16[16,256]{1,0:T(8,128)(2,1)} %interp.1, bf16[576,64]{1,0:T(8,128)(2,1)} %bitcast.7, f32[1,64]{1,0:T(1,128)} %bitcast.8), custom_call_target="tpu_custom_call" | custom-call | tf_op jit(solution)/shard_map/convolve/pallas_call | solution.py:350
Async XLA Ops:
  0.8 1.6 %copy-start = (bf16[960,1104]{1,0:T(8,128)(2,1)S(1)}, bf16[960,1104]{1,0:T(8,128)(2,1)}, u32[]{:S(2)}) copy-start(bf16[960,1104]{1,0:T(8,128)(2,1)} %coarse.1) | copy-start | bytes 6359044
  2.5 0.8 %copy-start.2 = (s32[32,144]{1,0:T(8,128)S(1)}, s32[32,144]{1,0:T(8,128)}, u32[]{:S(2)}) copy-start(s32[32,144]{1,0:T(8,128)} %ids.5) | copy-start | bytes 55300
  5.7 0.7 %copy-start.1 = (bf16[160,8,128]{2,1,0:T(8,128)(2,1)}, bf16[160,8,128]{2,1,0:T(8,128)(2,1)S(1)}, u32[]{:S(2)}) copy-start(bf16[160,8,128]{2,1,0:T(8,128)(2,1)S(1)} %pack.1) | copy-start | bytes 983044
  30.7 4.2 %collective-permute-start = (bf16[20,8,128]{2,1,0:T(8,128)(2,1)S(1)}, bf16[20,8,128]{2,1,0:T(8,128)(2,1)S(1)}, u32[]{:S(2)}, u32[]{:S(2)}) collective-permute-start(bf16[20,8,128]{2,1,0:T(8,128)(2,1)S(1)} %get-tuple-element.5), channel_id=1, source_target_pairs={{0,1},{1,2},{2,3},{3,4},{4,5},{5,6},{6,7},{8,9},{9,10},{10,11},{11... | collective-permute-start | bytes 122888 | tf_op jit(solution)/shard_map/ppermute | solution.py:343
  33.3 5.9 %collective-permute-start.1 = (bf16[20,8,128]{2,1,0:T(8,128)(2,1)S(1)}, bf16[20,8,128]{2,1,0:T(8,128)(2,1)S(1)}, u32[]{:S(2)}, u32[]{:S(2)}) collective-permute-start(bf16[20,8,128]{2,1,0:T(8,128)(2,1)S(1)} %get-tuple-element.6), channel_id=1, source_target_pairs={{1,0},{2,1},{3,2},{4,3},{5,4},{6,5},{7,6},{9,8},{10,9},{11,10},{12... | collective-permute-start | bytes 122888 | tf_op jit(solution)/shard_map/ppermute | solution.py:343
